TPU v7x, 128 devices: a whole 4x4x4 slice. The times are simulated.
128 devices in a mesh: row: 8 (over z, x_lo), col: 16 (over y, x_hi, core).
Axes of the slice: x: 4 (x_hi: 2, x_lo: 2; x = x_hi * 2 + x_lo), y: 4, z: 4, core: 2. Of those that a mesh axis runs over, the one named last changes fastest.
Arguments:
- normal_matrix: float32 [14336, 14336], P(('row', 'col')), may hold values from -90 to 90, as said below
- new_index: int32 [14336], replicated, may hold values from 0 to 14335, each once
- check_vectors: float32 [14336, 1024], P('col'), may hold values from -0.046875 to 0.046875
Outputs:
- tile_layout: float32 [14336, 14336], P('row', 'col')
- check_product: float32 [14336, 1024], P(('row', 'col'))
Inputs may be any that keep to these rules, and one draw needn't show every extreme that they name: normal_matrix is symmetric. new_index[a] is the new index of parameter a; every index 0 to 14335 appears once.
All inputs are finite; a program needn't handle non-finite values.
Results may differ from a plain program's by a relative error of at most 0.000082.
Values sent between devices are 32-bit elements; how exact they have to be, the bound alone decides.
No kernel may reach another device: no remote copies, remote signals or barrier semaphores. Data moves between devices by JAX's collectives and lax.ppermute only.
A program may use at most 128 MiB of HBM per device.

v0:
```python
import jax
import jax.numpy as jnp
from jax import lax
from jax.experimental import pallas as pl
from jax.experimental.pallas import tpu as pltpu
from jax.sharding import PartitionSpec as P


TILE = 128
LANES = 128
SUB = 8
VMEM = 24 * 1024 * 1024
SPANS = (48, 40, 24)
STEPS = 8


def params():
    return pltpu.CompilerParams(vmem_limit_bytes=VMEM)


def group_columns(slab, places, devices):
    share, unknowns = slab.shape
    steps, _, width = places.shape
    keep = share - SUB
    chunk = LANES - share

    def kernel(pos_ref, x_ref, out_ref, turned, spread):
        step = pl.program_id(0)

        for b in range(width // LANES + 1):
            if b < width // LANES:
                turned[b * LANES:(b + 1) * LANES, :share] = x_ref[:, b * LANES:(b + 1) * LANES].T
            if b > 0:
                for u in range((b - 1) * LANES, b * LANES):
                    spread[pl.ds(pos_ref[0, 0, u], 1), :] = turned[u:u + 1, :]

        @pl.when(step == steps - 1)
        def _():
            def pack(i, carry):
                for u in range(16):
                    b = i * 16 + u
                    x = spread[pl.ds(pl.multiple_of(b * share, SUB), share), :].T
                    out_ref[b, :, :share] = x[:keep]
                    for k in range(share // chunk):
                        out_ref[b, SUB * k:SUB * k + SUB, share:] = x[keep:share, chunk * k:chunk * (k + 1)]
                return carry

            lax.fori_loop(0, devices // 16, pack, 0)

    return pl.pallas_call(
        kernel,
        grid=(steps,),
        in_specs=[
            pl.BlockSpec((1, 1, width), lambda g: (g, 0, 0), memory_space=pltpu.SMEM),
            pl.BlockSpec((share, width), lambda g: (0, g)),
        ],
        out_specs=pl.BlockSpec(memory_space=pltpu.VMEM),
        scratch_shapes=[
            pltpu.VMEM((width, LANES), jnp.float32),
            pltpu.VMEM((unknowns, LANES), jnp.float32),
        ],
        out_shape=pltpu.VMEM((devices, keep, LANES), jnp.float32),
        compiler_params=params(),
        name="group_columns",
    )(places, slab)


def group_rows(blocks, places, groups, share, widths):
    devices, keep, _ = blocks.shape
    unknowns = devices * share
    chunk = LANES - share
    steps = places.shape[0]
    per = devices // steps
    rows = unknowns // groups
    starts = [sum(widths[:i]) for i in range(len(widths))]
    outs = 4
    each = groups // outs

    def kernel(pos_ref, x_ref, *refs):
        out_refs, (extra, spread) = refs[:-2], refs[-2:]
        step = pl.program_id(0)

        @pl.when(step < steps)
        def _():
            for b in range(per):
                start = b * share
                for k in range(share // chunk):
                    extra[b * SUB:(b + 1) * SUB, chunk * k:chunk * (k + 1)] = x_ref[b, SUB * k:SUB * k + SUB, share:]
                for u in range(keep):
                    spread[pl.ds(pos_ref[0, 0, start + u], 1), :] = x_ref[b, u:u + 1, :]
                for u in range(SUB):
                    at = b * SUB + u
                    spread[pl.ds(pos_ref[0, 0, start + keep + u], 1), :] = extra[at:at + 1, :]

        @pl.when(step >= steps)
        def _():
            def turn(e, carry):
                g = (step - steps) * each + e
                for ref, start, width in zip(out_refs, starts, widths):
                    for k in range(width // LANES):
                        at = pl.multiple_of(g * rows + start + k * LANES, LANES)
                        ref[e, :, k * LANES:(k + 1) * LANES] = spread[pl.ds(at, LANES), :].T[:share]
                return carry

            lax.fori_loop(0, each, turn, 0)

    late = lambda g: (jnp.maximum(g - steps, 0), 0, 0)
    early = lambda g: (jnp.minimum(g, steps - 1), 0, 0)
    return pl.pallas_call(
        kernel,
        grid=(steps + outs,),
        in_specs=[
            pl.BlockSpec((1, 1, per * share), early, memory_space=pltpu.SMEM),
            pl.BlockSpec((per, keep, LANES), early),
        ],
        out_specs=[pl.BlockSpec((each, share, w), late) for w in widths],
        scratch_shapes=[
            pltpu.VMEM((per * SUB, LANES), jnp.float32),
            pltpu.VMEM((unknowns, LANES), jnp.float32),
        ],
        out_shape=[pltpu.HBM((groups, share, w), jnp.float32) for w in widths],
        compiler_params=params(),
        name="group_rows",
    )(places, blocks)


def tile_and_product(turned, v_hi, v_lo, where, tile, cols, share, offset):
    groups, _, rows = turned.shape
    span = rows // cols
    columns, width = v_hi.shape
    steps = 4
    wide = width // steps
    pairs = cols // 2

    def kernel(where_ref, x_ref, hi_ref, lo_ref, *refs):
        tile_ref, other_ref, mine_ref, x_in, x_hi, x_lo, held, x_sem, sem = refs[-9:]
        step = pl.program_id(0)
        store = pltpu.make_async_copy(held, tile_ref.at[:, offset:offset + span, :], sem)

        @pl.when(step == 0)
        def _():
            fetch = pltpu.make_async_copy(x_ref, x_in, x_sem)
            fetch.start()
            fetch.wait()
            for k in range(rows // LANES):
                x = x_in[:, :, k * LANES:(k + 1) * LANES].reshape(columns, LANES).T
                hi = x.astype(jnp.bfloat16)
                x_hi[k * LANES:(k + 1) * LANES, :] = hi
                x_lo[k * LANES:(k + 1) * LANES, :] = (x - hi.astype(jnp.float32)).astype(jnp.bfloat16)
                for s in range(0, LANES, SUB):
                    c, m = divmod(k * LANES + s, span)
                    held[c, m:m + SUB, :] = x[s:s + SUB]
            store.start()

        part = (
            jnp.dot(x_hi[...], hi_ref[...], preferred_element_type=jnp.float32)
            + jnp.dot(x_hi[...], lo_ref[...], preferred_element_type=jnp.float32)
            + jnp.dot(x_lo[...], hi_ref[...], preferred_element_type=jnp.float32)
        )
        even = where_ref[0] == 0
        for c in range(pairs):
            slot = c ^ where_ref[1]
            first = part[2 * c * span:(2 * c + 1) * span]
            second = part[(2 * c + 1) * span:(2 * c + 2) * span]
            other_ref[slot] = jnp.where(even, second, first)
            mine_ref[slot] = jnp.where(even, first, second)

        @pl.when(step == steps - 1)
        def _():
            store.wait()

    half = jax.ShapeDtypeStruct((pairs, span, width), jnp.float32)
    half_spec = pl.BlockSpec((pairs, span, wide), lambda g, where: (0, 0, g))
    in_specs = [pl.BlockSpec(memory_space=pl.ANY)]
    in_specs += [pl.BlockSpec((columns, wide), lambda g, where: (0, g))] * 2
    operands = [where, turned, v_hi, v_lo]
    aliases = {}
    if tile is not None:
        aliases = {len(operands): 0}
        operands.append(tile)
        in_specs.append(pl.BlockSpec(memory_space=pl.ANY))
    return pl.pallas_call(
        kernel,
        grid_spec=pltpu.PrefetchScalarGridSpec(
            num_scalar_prefetch=1,
            grid=(steps,),
            in_specs=in_specs,
            out_specs=[pl.BlockSpec(memory_space=pl.ANY), half_spec, half_spec],
            scratch_shapes=[
                pltpu.VMEM((groups, share, rows), jnp.float32),
                pltpu.VMEM((rows, columns), jnp.bfloat16),
                pltpu.VMEM((rows, columns), jnp.bfloat16),
                pltpu.VMEM((cols, span, columns), jnp.float32),
                pltpu.SemaphoreType.DMA,
                pltpu.SemaphoreType.DMA,
            ],
        ),
        out_shape=[jax.ShapeDtypeStruct((cols, share, columns), jnp.float32), half, half],
        input_output_aliases=aliases,
        compiler_params=params(),
        cost_estimate=pl.CostEstimate(flops=6 * rows * columns * width, bytes_accessed=8 * rows * columns, transcendentals=0),
    )(*operands)


def shards(normal_matrix, new_index, check_vectors):
    row_count = lax.axis_size("row")
    col_count = lax.axis_size("col")
    devices = row_count * col_count
    share, unknowns = normal_matrix.shape
    rows = unknowns // row_count
    steps = STEPS

    tile, lane = new_index // TILE, new_index % TILE
    within_col = tile // col_count * TILE + lane
    column_places = (within_col // share * col_count + tile % col_count) * share + within_col % share
    within_row = tile // row_count * TILE + lane
    owner, m = within_row // share, within_row % share
    spot = jnp.zeros_like(m)
    start = 0
    for span in SPANS:
        spot = jnp.where((m >= start) & (m < start + span), start * col_count + owner * span + m - start, spot)
        start += span
    row_places = tile % row_count * rows + spot
    column_places = column_places.reshape(steps, 1, unknowns // steps)
    row_places = row_places.reshape(steps, 1, unknowns // steps)

    along = lambda x: lax.all_to_all(x, "row", split_axis=0, concat_axis=0, tiled=True)
    flip = lambda x, bits: lax.ppermute(x, "col", [(i, i ^ bits) for i in range(col_count)])
    groups = [list(range(p, col_count, 2)) for p in range(2)]
    widths = [s * col_count for s in SPANS]

    in_hbm = lambda x: pltpu.with_memory_space_constraint(x, pltpu.HBM)
    outgoing = group_columns(in_hbm(normal_matrix), column_places, devices)
    arrived = lax.all_to_all(outgoing, ("row", "col"), split_axis=0, concat_axis=0, tiled=True)
    v_hi = lax.reduce_precision(check_vectors, 8, 7)
    v_lo = (check_vectors - v_hi).astype(jnp.bfloat16)
    v_hi = v_hi.astype(jnp.bfloat16)
    me = lax.axis_index("col").astype(jnp.int32)

    chosen = group_rows(arrived, row_places, row_count, share, widths)

    tile_layout = None
    sums = []
    last, held = arrived, None
    offset = 0
    for q, span in enumerate(SPANS):
        final = q == len(SPANS) - 1
        send, _ = lax.optimization_barrier((chosen[q], last))
        last = along(send)
        piece = last
        seat = me
        if held is not None:
            piece, _ = lax.optimization_barrier((last, held))
            seat, _ = lax.optimization_barrier((me, held))
        where = jnp.stack([seat % 2, jnp.zeros_like(seat) if final else seat // 2])
        tile_layout, other, mine = tile_and_product(
            piece, in_hbm(v_hi), in_hbm(v_lo), where, tile_layout, col_count, share, offset
        )
        offset += span
        theirs = flip(other, 1)
        if final:
            both = mine + theirs
            parts = lax.all_to_all(both, "col", split_axis=0, concat_axis=0, axis_index_groups=groups, tiled=True)
            sums.append(parts.sum(axis=0))
        else:
            both = [mine[i:i + 2] + theirs[i:i + 2] for i in range(0, col_count // 2, 2)]
            near = both[0]
            for y in range(1, col_count // 4):
                got = flip(both[y], 4 * y)
                near = near + got
            held = tuple(both[1:])
            got = flip(near[1], 2)
            sums.append(near[0] + got)
    return tile_layout.reshape(rows, unknowns // col_count), jnp.concatenate(sums, axis=0)


def solution(mesh):
    return jax.shard_map(
        shards,
        mesh=mesh,
        in_specs=(P(("row", "col"), None), P(), P("col", None)),
        out_specs=(P("row", "col"), P(("row", "col"), None)),
        check_vma=False,
    )
```

profile of v0, /device:TPU:0, one launch (start us, length us, event | category | flops | bytes accessed | tf_op | source)
XLA Modules:
  0.0 278.0 jit_solution(17594334211020613241)
XLA Ops:
  0.6 1.1 fusion.18
  1.8 17.0 %group_columns.1 = f32[128,104,128]{2,1,0:T(8,128)S(1)} custom-call(s32[8,1,1792]{2,1,0:T(1,128)S(1)} %bitcast.21, f32[112,14336]{1,0:T(8,128)} %x_ref.1), custom_call_target="tpu_custom_call" | custom-call | tf_op jit(solution)/shard_map/group_columns/pallas_call | solution.py:50
  18.8 91.3 %all_to_all.25.x_ref = f32[128,104,128]{2,1,0:T(8,128)S(1)} all-to-all(f32[128,104,128]{2,1,0:T(8,128)S(1)} %group_columns.1), channel_id=1, replica_groups=mesh['row'=8,'col'=16] {'row','col'}, dimensions={0} | all-to-all | bytes 13631488 | tf_op jit(solution)/shard_map/all_to_all | solution.py:234
  110.1 17.6 %group_rows.1 = (f32[8,112,768]{2,1,0:T(8,128)}, f32[8,112,640]{2,1,0:T(8,128)}, f32[8,112,384]{2,1,0:T(8,128)}) custom-call(s32[8,1,1792]{2,1,0:T(1,128)S(1)} %bitcast.20, f32[128,104,128]{2,1,0:T(8,128)S(1)} %all_to_all.25.x_ref), custom_call_target="tpu_custom_call" | custom-call | tf_op jit(solution)/shard_map/group_rows/pallas_call | solution.py:109
  127.7 3.6 %all-to-all-start.1 = ((f32[8,112,768]{2,1,0:T(8,128)}), f32[8,112,768]{2,1,0:T(8,128)S(1)}, u32[]{:S(2)}, u32[]{:S(2)}) async-start(f32[8,112,768]{2,1,0:T(8,128)} %get-tuple-element.22), calls=%async_computation.1 | async-start | bytes 5505024 | tf_op jit(solution)/shard_map/all_to_all | solution.py:227
  131.3 0.1 pad_add_fusion.where_ref
  131.4 4.7 %fusion = (bf16[896,1024]{1,0:T(8,128)(2,1)}, bf16[896,1024]{1,0:T(8,128)(2,1)}) fusion(f32[896,1024]{1,0:T(8,128)} %param.5), kind=kLoop, calls=%fused_computation.2 | loop fusion | flops 3670016 | bytes 7340032 | tf_op jit(solution)/shard_map/convert_element_type | solution.py:236
  136.1 29.2 %all-to-all-done.1.x_ref = f32[8,112,768]{2,1,0:T(8,128)S(1)} async-done(((f32[8,112,768]{2,1,0:T(8,128)}), f32[8,112,768]{2,1,0:T(8,128)S(1)}, u32[]{:S(2)}, u32[]{:S(2)}) %all-to-all-start.1) | async-done | bytes 2752544 | tf_op jit(solution)/shard_map/all_to_all | solution.py:227
  165.4 4.4 %all-to-all-start.2 = ((f32[8,112,640]{2,1,0:T(8,128)}), f32[8,112,640]{2,1,0:T(8,128)}, u32[]{:S(2)}, u32[]{:S(2)}) async-start(f32[8,112,640]{2,1,0:T(8,128)} %get-tuple-element.27), calls=%async_computation.2 | async-start | bytes 4587520 | tf_op jit(solution)/shard_map/all_to_all | solution.py:227
  169.7 8.9 %shard_map.50 = (f32[16,112,896]{2,1,0:T(8,128)}, f32[8,48,1024]{2,1,0:T(8,128)S(1)}, f32[8,48,1024]{2,1,0:T(8,128)S(1)}) custom-call(s32[2]{0:T(128)S(1)} %pad_add_fusion.where_ref, f32[8,112,768]{2,1,0:T(8,128)S(1)} %all-to-all-done.1.x_ref, bf16[896,1024]{1,0:T(8,128)(2,1)} %get-tuple-element.41.hi_ref, bf16[896,1024]{1,0:T(8,128)(2,1)} %get-tuple-element.40.lo_ref), custom_call_target="tpu_custom_call" | custom-call | flops 4227858432 | bytes 5505024 | tf_op jit(solution)/shard_map/pallas_call | solution.py:182
  178.6 0.1 collective-permute-start
  178.7 3.4 %collective-permute-done = f32[8,48,1024]{2,1,0:T(8,128)S(1)} collective-permute-done((f32[8,48,1024]{2,1,0:T(8,128)S(1)}, f32[8,48,1024]{2,1,0:T(8,128)S(1)}, u32[]{:S(2)}, u32[]{:S(2)}) %collective-permute-start) | collective-permute-done | bytes 1572896 | tf_op jit(solution)/shard_map/ppermute | solution.py:228
  182.1 1.2 slice_add_fusion.1
  183.3 0.1 copy-done.1
  183.4 0.1 pad_add_fusion.1.where_ref
  183.5 14.6 %all-to-all-done.2.x_ref = f32[8,112,640]{2,1,0:T(8,128)} async-done(((f32[8,112,640]{2,1,0:T(8,128)}), f32[8,112,640]{2,1,0:T(8,128)}, u32[]{:S(2)}, u32[]{:S(2)}) %all-to-all-start.2) | async-done | bytes 2293792 | tf_op jit(solution)/shard_map/all_to_all | solution.py:227
  198.1 9.9 %shard_map.51 = (f32[16,112,896]{2,1,0:T(8,128)}, f32[8,40,1024]{2,1,0:T(8,128)}, f32[8,40,1024]{2,1,0:T(8,128)S(1)}) custom-call(s32[2]{0:T(128)S(1)} %pad_add_fusion.1.where_ref, f32[8,112,640]{2,1,0:T(8,128)} %all-to-all-done.2.x_ref, bf16[896,1024]{1,0:T(8,128)(2,1)} %get-tuple-element.41.hi_ref, ...), custom_call_target="tpu_custom_call", output_to_operand_aliasing={{0}: (4, {})} | custom-call | flops 3523215360 | bytes 4587520 | tf_op jit(solution)/shard_map/pallas_call | solution.py:182
  208.0 0.1 collective-permute-start.1
  208.1 3.6 %all-to-all-start.3 = ((f32[8,112,384]{2,1,0:T(8,128)}), f32[8,112,384]{2,1,0:T(8,128)S(1)}, u32[]{:S(2)}, u32[]{:S(2)}) async-start(f32[8,112,384]{2,1,0:T(8,128)} %get-tuple-element.34), calls=%async_computation.3 | async-start | bytes 2752512 | tf_op jit(solution)/shard_map/all_to_all | solution.py:227
  211.7 0.1 collective-permute-start.2
  211.8 4.0 %collective-permute-start.3 = (f32[2,48,1024]{2,1,0:T(8,128)S(1)}, f32[2,48,1024]{2,1,0:T(8,128)}, u32[]{:S(2)}, u32[]{:S(2)}) collective-permute-start(f32[2,48,1024]{2,1,0:T(8,128)S(1)} %get-tuple-element.43), channel_id=1, source_target_pairs={{0,8},{1,9},{2,10},{3,11},{4,12},{5,13},{6,14},{7,15},{8,0},{9,1},... | collective-permute-start | bytes 1179656 | tf_op jit(solution)/shard_map/ppermute | solution.py:228
  215.7 0.7 collective-permute-start.4
  216.5 0.0 collective-permute-done.1
  216.5 2.2 slice_add_fusion.5
  218.6 0.6 collective-permute-start.6
  219.2 3.4 %collective-permute-start.7 = (f32[2,40,1024]{2,1,0:T(8,128)}, f32[2,40,1024]{2,1,0:T(8,128)}, u32[]{:S(2)}, u32[]{:S(2)}) collective-permute-start(f32[2,40,1024]{2,1,0:T(8,128)} %get-tuple-element.46), channel_id=1, source_target_pairs={{0,8},{1,9},{2,10},{3,11},{4,12},{5,13},{6,14},{7,15},{8,0},{9,1},... | collective-permute-start | bytes 983048 | tf_op jit(solution)/shard_map/ppermute | solution.py:228
  222.6 9.2 %all-to-all-done.3.x_ref = f32[8,112,384]{2,1,0:T(8,128)S(1)} async-done(((f32[8,112,384]{2,1,0:T(8,128)}), f32[8,112,384]{2,1,0:T(8,128)S(1)}, u32[]{:S(2)}, u32[]{:S(2)}) %all-to-all-start.3) | async-done | bytes 1376288 | tf_op jit(solution)/shard_map/all_to_all | solution.py:227
  231.8 0.1 pad_add_fusion.2.where_ref
  231.9 6.1 %shard_map.52 = (f32[16,112,896]{2,1,0:T(8,128)}, f32[8,24,1024]{2,1,0:T(8,128)S(1)}, f32[8,24,1024]{2,1,0:T(8,128)S(1)}) custom-call(s32[2]{0:T(128)S(1)} %pad_add_fusion.2.where_ref, f32[8,112,384]{2,1,0:T(8,128)S(1)} %all-to-all-done.3.x_ref, bf16[896,1024]{1,0:T(8,128)(2,1)} %get-tuple-element.41.hi_ref, ...), custom_call_target="tpu_custom_call", output_to_operand_aliasing={{0}: (4, {})} | custom-call | flops 2113929216 | bytes 2752512 | tf_op jit(solution)/shard_map/pallas_call | solution.py:182
  238.0 0.0 collective-permute-done.2
  238.0 2.5 collective-permute-start.8
  240.5 0.0 collective-permute-done.3
  240.5 0.0 collective-permute-start.10
  240.5 0.0 collective-permute-done.4
  240.6 1.6 fusion.3
  242.2 0.1 collective-permute-start.5
  242.3 0.0 collective-permute-done.6
  242.3 6.0 %collective-permute-done.7 = f32[2,40,1024]{2,1,0:T(8,128)} collective-permute-done((f32[2,40,1024]{2,1,0:T(8,128)}, f32[2,40,1024]{2,1,0:T(8,128)}, u32[]{:S(2)}, u32[]{:S(2)}) %collective-permute-start.7) | collective-permute-done | bytes 327712 | tf_op jit(solution)/shard_map/ppermute | solution.py:228
  248.3 6.8 %collective-permute-done.8 = f32[2,40,1024]{2,1,0:T(8,128)S(1)} collective-permute-done((f32[2,40,1024]{2,1,0:T(8,128)S(1)}, f32[2,40,1024]{2,1,0:T(8,128)S(1)}, u32[]{:S(2)}, u32[]{:S(2)}) %collective-permute-start.8) | collective-permute-done | bytes 327712 | tf_op jit(solution)/shard_map/ppermute | solution.py:228
  255.1 1.3 fusion.6
  256.4 0.0 collective-permute-done.10
  256.4 1.0 add.164
  257.4 3.5 %all-to-all-start.4 = ((f32[8,24,1024]{2,1,0:T(8,128)}), f32[8,24,1024]{2,1,0:T(8,128)S(1)}, u32[]{:S(2)}, u32[]{:S(2)}) async-start(f32[8,24,1024]{2,1,0:T(8,128)} %add.164), calls=%async_computation.4 | async-start | bytes 1572864 | tf_op jit(solution)/shard_map/all_to_all | solution.py:263
  261.0 3.5 %collective-permute-start.9 = (f32[40,1024]{1,0:T(8,128)S(1)}, f32[40,1024]{1,0:T(8,128)S(1)}, u32[]{:S(2)}, u32[]{:S(2)}) collective-permute-start(f32[40,1024]{1,0:T(8,128)S(1)} %slice_bitcast_fusion.2), channel_id=1, source_target_pairs={{0,2},{1,3},{2,0},{3,1},{4,6},{5,7},{6,4},{7,5},{8,10},{9,11},{10,... | collective-permute-start | bytes 491528 | tf_op jit(solution)/shard_map/ppermute | solution.py:228
  264.5 0.0 collective-permute-done.5
  264.5 12.6 %collective-permute-done.9 = f32[40,1024]{1,0:T(8,128)S(1)} collective-permute-done((f32[40,1024]{1,0:T(8,128)S(1)}, f32[40,1024]{1,0:T(8,128)S(1)}, u32[]{:S(2)}, u32[]{:S(2)}) %collective-permute-start.9) | collective-permute-done | bytes 163872 | tf_op jit(solution)/shard_map/ppermute | solution.py:228
  277.2 0.0 all-to-all-done.4
  277.2 0.8 pad_maximum_fusion
  (10 shorter events, 0.1 us)
Async XLA Ops:
  127.7 37.7 %all-to-all-start.1 = ((f32[8,112,768]{2,1,0:T(8,128)}), f32[8,112,768]{2,1,0:T(8,128)S(1)}, u32[]{:S(2)}, u32[]{:S(2)}) async-start(f32[8,112,768]{2,1,0:T(8,128)} %get-tuple-element.22), calls=%async_computation.1 | async-start | bytes 5505024 | tf_op jit(solution)/shard_map/all_to_all | solution.py:227
  165.4 32.8 %all-to-all-start.2 = ((f32[8,112,640]{2,1,0:T(8,128)}), f32[8,112,640]{2,1,0:T(8,128)}, u32[]{:S(2)}, u32[]{:S(2)}) async-start(f32[8,112,640]{2,1,0:T(8,128)} %get-tuple-element.27), calls=%async_computation.2 | async-start | bytes 4587520 | tf_op jit(solution)/shard_map/all_to_all | solution.py:227
  178.6 3.5 %copy-start = (f32[8,48,1024]{2,1,0:T(8,128)}, f32[8,48,1024]{2,1,0:T(8,128)S(1)}, u32[]{:S(2)}) copy-start(f32[8,48,1024]{2,1,0:T(8,128)S(1)} %get-tuple-element.23) | copy-start | bytes 4718596
  178.6 3.5 %collective-permute-start = (f32[8,48,1024]{2,1,0:T(8,128)S(1)}, f32[8,48,1024]{2,1,0:T(8,128)S(1)}, u32[]{:S(2)}, u32[]{:S(2)}) collective-permute-start(f32[8,48,1024]{2,1,0:T(8,128)S(1)} %get-tuple-element.24), channel_id=1, source_target_pairs={{0,1},{1,0},{2,3},{3,2},{4,5},{5,4},{6,7},{7,6},{8,9},{9,8},{10,11... | collective-permute-start | bytes 4718600 | tf_op jit(solution)/shard_map/ppermute | solution.py:228
  182.1 1.3 copy-start.1
  208.0 8.5 %collective-permute-start.1 = (f32[8,40,1024]{2,1,0:T(8,128)}, f32[8,40,1024]{2,1,0:T(8,128)}, u32[]{:S(2)}, u32[]{:S(2)}) collective-permute-start(f32[8,40,1024]{2,1,0:T(8,128)} %get-tuple-element.31), channel_id=1, source_target_pairs={{0,1},{1,0},{2,3},{3,2},{4,5},{5,4},{6,7},{7,6},{8,9},{9,8},{10,11... | collective-permute-start | bytes 3932168 | tf_op jit(solution)/shard_map/ppermute | solution.py:228
  208.1 23.7 %all-to-all-start.3 = ((f32[8,112,384]{2,1,0:T(8,128)}), f32[8,112,384]{2,1,0:T(8,128)S(1)}, u32[]{:S(2)}, u32[]{:S(2)}) async-start(f32[8,112,384]{2,1,0:T(8,128)} %get-tuple-element.34), calls=%async_computation.3 | async-start | bytes 2752512 | tf_op jit(solution)/shard_map/all_to_all | solution.py:227
  211.7 26.3 %collective-permute-start.2 = (f32[2,48,1024]{2,1,0:T(8,128)}, f32[2,48,1024]{2,1,0:T(8,128)}, u32[]{:S(2)}, u32[]{:S(2)}) collective-permute-start(f32[2,48,1024]{2,1,0:T(8,128)} %get-tuple-element.44), channel_id=1, source_target_pairs={{0,4},{1,5},{2,6},{3,7},{4,0},{5,1},{6,2},{7,3},{8,12},{9,13},{10,... | collective-permute-start | bytes 1179656 | tf_op jit(solution)/shard_map/ppermute | solution.py:228
  211.8 28.8 %collective-permute-start.3 = (f32[2,48,1024]{2,1,0:T(8,128)S(1)}, f32[2,48,1024]{2,1,0:T(8,128)}, u32[]{:S(2)}, u32[]{:S(2)}) collective-permute-start(f32[2,48,1024]{2,1,0:T(8,128)S(1)} %get-tuple-element.43), channel_id=1, source_target_pairs={{0,8},{1,9},{2,10},{3,11},{4,12},{5,13},{6,14},{7,15},{8,0},{9,1},... | collective-permute-start | bytes 1179656 | tf_op jit(solution)/shard_map/ppermute | solution.py:228
  215.7 24.8 %collective-permute-start.4 = (f32[2,48,1024]{2,1,0:T(8,128)S(1)}, f32[2,48,1024]{2,1,0:T(8,128)}, u32[]{:S(2)}, u32[]{:S(2)}) collective-permute-start(f32[2,48,1024]{2,1,0:T(8,128)S(1)} %get-tuple-element.42), channel_id=1, source_target_pairs={{0,12},{1,13},{2,14},{3,15},{4,8},{5,9},{6,10},{7,11},{8,4},{9,5},... | collective-permute-start | bytes 1179656 | tf_op jit(solution)/shard_map/ppermute | solution.py:228
  218.6 23.7 %collective-permute-start.6 = (f32[2,40,1024]{2,1,0:T(8,128)}, f32[2,40,1024]{2,1,0:T(8,128)}, u32[]{:S(2)}, u32[]{:S(2)}) collective-permute-start(f32[2,40,1024]{2,1,0:T(8,128)} %get-tuple-element.47), channel_id=1, source_target_pairs={{0,4},{1,5},{2,6},{3,7},{4,0},{5,1},{6,2},{7,3},{8,12},{9,13},{10,... | collective-permute-start | bytes 983048 | tf_op jit(solution)/shard_map/ppermute | solution.py:228
  219.2 29.1 %collective-permute-start.7 = (f32[2,40,1024]{2,1,0:T(8,128)}, f32[2,40,1024]{2,1,0:T(8,128)}, u32[]{:S(2)}, u32[]{:S(2)}) collective-permute-start(f32[2,40,1024]{2,1,0:T(8,128)} %get-tuple-element.46), channel_id=1, source_target_pairs={{0,8},{1,9},{2,10},{3,11},{4,12},{5,13},{6,14},{7,15},{8,0},{9,1},... | collective-permute-start | bytes 983048 | tf_op jit(solution)/shard_map/ppermute | solution.py:228
  231.9 6.1 %copy-start.2 = (f32[2,40,1024]{2,1,0:T(8,128)S(1)}, f32[2,40,1024]{2,1,0:T(8,128)}, u32[]{:S(2)}) copy-start(f32[2,40,1024]{2,1,0:T(8,128)} %get-tuple-element.45) | copy-start | bytes 983044
  238.0 17.2 %collective-permute-start.8 = (f32[2,40,1024]{2,1,0:T(8,128)S(1)}, f32[2,40,1024]{2,1,0:T(8,128)S(1)}, u32[]{:S(2)}, u32[]{:S(2)}) collective-permute-start(f32[2,40,1024]{2,1,0:T(8,128)S(1)} %copy-done.2), channel_id=1, source_target_pairs={{0,12},{1,13},{2,14},{3,15},{4,8},{5,9},{6,10},{7,11},{8,4},{9,5},... | collective-permute-start | bytes 983048 | tf_op jit(solution)/shard_map/ppermute | solution.py:228
  240.5 15.9 %collective-permute-start.10 = (f32[8,24,1024]{2,1,0:T(8,128)S(1)}, f32[8,24,1024]{2,1,0:T(8,128)S(1)}, u32[]{:S(2)}, u32[]{:S(2)}) collective-permute-start(f32[8,24,1024]{2,1,0:T(8,128)S(1)} %get-tuple-element.39), channel_id=1, source_target_pairs={{0,1},{1,0},{2,3},{3,2},{4,5},{5,4},{6,7},{7,6},{8,9},{9,8},{10,11... | collective-permute-start | bytes 2359304 | tf_op jit(solution)/shard_map/ppermute | solution.py:228
  242.2 22.3 %collective-permute-start.5 = (f32[48,1024]{1,0:T(8,128)S(1)}, f32[48,1024]{1,0:T(8,128)S(1)}, u32[]{:S(2)}, u32[]{:S(2)}) collective-permute-start(f32[48,1024]{1,0:T(8,128)S(1)} %slice_bitcast_fusion), channel_id=1, source_target_pairs={{0,2},{1,3},{2,0},{3,1},{4,6},{5,7},{6,4},{7,5},{8,10},{9,11},{10,... | collective-permute-start | bytes 589832 | tf_op jit(solution)/shard_map/ppermute | solution.py:228
  257.4 19.7 %all-to-all-start.4 = ((f32[8,24,1024]{2,1,0:T(8,128)}), f32[8,24,1024]{2,1,0:T(8,128)S(1)}, u32[]{:S(2)}, u32[]{:S(2)}) async-start(f32[8,24,1024]{2,1,0:T(8,128)} %add.164), calls=%async_computation.4 | async-start | bytes 1572864 | tf_op jit(solution)/shard_map/all_to_all | solution.py:263
  261.0 16.1 %collective-permute-start.9 = (f32[40,1024]{1,0:T(8,128)S(1)}, f32[40,1024]{1,0:T(8,128)S(1)}, u32[]{:S(2)}, u32[]{:S(2)}) collective-permute-start(f32[40,1024]{1,0:T(8,128)S(1)} %slice_bitcast_fusion.2), channel_id=1, source_target_pairs={{0,2},{1,3},{2,0},{3,1},{4,6},{5,7},{6,4},{7,5},{8,10},{9,11},{10,... | collective-permute-start | bytes 491528 | tf_op jit(solution)/shard_map/ppermute | solution.py:228
where the time goes:
time: 279 us; the launch traced here: 278 us
  blocking collectives  91.3 us (33%)
  waiting for transfers between devices  82 us (29%)
  Pallas kernels  59.4 us (21%)
  starting transfers between devices  30.2 us (11%)
  other arithmetic  14.2 us (5%)
    all_to_all x1, blocking collectives, shards(): lax.all_to_all(outgoing, ('row', 'col'), split_axis=0, concat_axis=0, til...  91.3 us
    all_to_all x3, waiting for transfers between devices, shards(): lax.all_to_all(x, 'row', split_axis=0, concat_axis=0, tiled=True)  53.1 us
    ppermute x11, waiting for transfers between devices, shards(): lax.ppermute(x, 'col', [(i, i ^ bits) for i in range(col_count)])  28.9 us
    pallas_call x3, Pallas kernels, tile_and_product(): pl.pallas_call(kernel, grid_spec=pltpu.PrefetchScalarGridSpec(num_scalar_...  24.8 us
    pallas_call x1, Pallas kernels, group_rows(): pl.pallas_call(kernel, grid=(steps + outs,), in_specs=[pl.BlockSpec((1, 1...  17.6 us
    pallas_call x1, Pallas kernels, group_columns(): pl.pallas_call(kernel, grid=(steps,), in_specs=[pl.BlockSpec((1, 1, width...  17 us
    ppermute x11, starting transfers between devices, shards(): lax.ppermute(x, 'col', [(i, i ^ bits) for i in range(col_count)])  15 us
    all_to_all x3, starting transfers between devices, shards(): lax.all_to_all(x, 'row', split_axis=0, concat_axis=0, tiled=True)  11.6 us
  transfers between devices with their start and end apart: 15, of which 7 were waited for; matrix products, arithmetic and copies ran while one was open for 4% of the time, Pallas kernels for 5%

commit v1 on v0

--- a/solution.py
+++ b/solution.py
@@ -128,7 +128,7 @@
     groups, _, rows = turned.shape
     span = rows // cols
     columns, width = v_hi.shape
-    steps = 4
+    steps = 2
     wide = width // steps
     pairs = cols // 2
 
@@ -139,10 +139,14 @@
 
         @pl.when(step == 0)
         def _():
-            fetch = pltpu.make_async_copy(x_ref, x_in, x_sem)
-            fetch.start()
-            fetch.wait()
+            parts = [slice(k * LANES, (k + 1) * LANES) for k in range(rows // LANES)]
+            fetches = [
+                pltpu.make_async_copy(x_ref.at[:, :, p], x_in.at[:, :, p], x_sem.at[k]) for k, p in enumerate(parts)
+            ]
+            for fetch in fetches:
+                fetch.start()
             for k in range(rows // LANES):
+                fetches[k].wait()
                 x = x_in[:, :, k * LANES:(k + 1) * LANES].reshape(columns, LANES).T
                 hi = x.astype(jnp.bfloat16)
                 x_hi[k * LANES:(k + 1) * LANES, :] = hi
@@ -191,7 +195,7 @@
                 pltpu.VMEM((rows, columns), jnp.bfloat16),
                 pltpu.VMEM((rows, columns), jnp.bfloat16),
                 pltpu.VMEM((cols, span, columns), jnp.float32),
-                pltpu.SemaphoreType.DMA,
+                pltpu.SemaphoreType.DMA((rows // LANES,)),
                 pltpu.SemaphoreType.DMA,
             ],
         ),
@@ -264,6 +268,7 @@
             sums.append(parts.sum(axis=0))
         else:
             both = [mine[i:i + 2] + theirs[i:i + 2] for i in range(0, col_count // 2, 2)]
+            both = lax.optimization_barrier(tuple(both))
             near = both[0]
             for y in range(1, col_count // 4):
                 got = flip(both[y], 4 * y)

time: 279 us -> 281 us (level)
  waiting for transfers between devices: 82 us -> 86 us
    all_to_all x3, waiting for transfers between devices: 53.1 us -> 57 us  [shards(): lax.all_to_all(x, 'row', split_axis=0, concat_axis=0, tiled=True)]
  transfers between devices with their start and end apart: 15 -> 15, of which waited for: 7 -> 9; matrix products, arithmetic and copies ran while one was open for 4% -> 4% of each run, Pallas kernels for 5% -> 5%
where the time goes in v1:
time: 281 us
  blocking collectives  91.3 us (32%)
  waiting for transfers between devices  86 us (31%)
  Pallas kernels  58.7 us (21%)
  starting transfers between devices  29.9 us (11%)
  other arithmetic  13.7 us (5%)
    all_to_all x1, blocking collectives, shards(): lax.all_to_all(outgoing, ('row', 'col'), split_axis=0, concat_axis=0, til...  91.3 us
    all_to_all x3, waiting for transfers between devices, shards(): lax.all_to_all(x, 'row', split_axis=0, concat_axis=0, tiled=True)  57 us
    ppermute x11, waiting for transfers between devices, shards(): lax.ppermute(x, 'col', [(i, i ^ bits) for i in range(col_count)])  28.7 us
    pallas_call x3, Pallas kernels, tile_and_product(): pl.pallas_call(kernel, grid_spec=pltpu.PrefetchScalarGridSpec(num_scalar_...  24.2 us
    pallas_call x1, Pallas kernels, group_rows(): pl.pallas_call(kernel, grid=(steps + outs,), in_specs=[pl.BlockSpec((1, 1...  17.6 us
    pallas_call x1, Pallas kernels, group_columns(): pl.pallas_call(kernel, grid=(steps,), in_specs=[pl.BlockSpec((1, 1, width...  17 us
    ppermute x11, starting transfers between devices, shards(): lax.ppermute(x, 'col', [(i, i ^ bits) for i in range(col_count)])  14.8 us
    all_to_all x3, starting transfers between devices, shards(): lax.all_to_all(x, 'row', split_axis=0, concat_axis=0, tiled=True)  11.6 us
  transfers between devices with their start and end apart: 15, of which 9 were waited for; matrix products, arithmetic and copies ran while one was open for 4% of the time, Pallas kernels for 5%

profile of v1, /device:TPU:0, one launch (start us, length us, event | category | flops | bytes accessed | tf_op | source)
XLA Modules:
  0.0 280.6 jit_solution(766543835852278509)
XLA Ops:
  0.6 1.1 fusion.12
  1.8 17.0 %group_columns.1 = f32[128,104,128]{2,1,0:T(8,128)S(1)} custom-call(s32[8,1,1792]{2,1,0:T(1,128)S(1)} %bitcast.21, f32[112,14336]{1,0:T(8,128)} %x_ref.1), custom_call_target="tpu_custom_call" | custom-call | tf_op jit(solution)/shard_map/group_columns/pallas_call | solution.py:50
  18.8 91.3 %all_to_all.25.x_ref = f32[128,104,128]{2,1,0:T(8,128)S(1)} all-to-all(f32[128,104,128]{2,1,0:T(8,128)S(1)} %group_columns.1), channel_id=1, replica_groups=mesh['row'=8,'col'=16] {'row','col'}, dimensions={0} | all-to-all | bytes 13631488 | tf_op jit(solution)/shard_map/all_to_all | solution.py:238
  110.1 17.6 %group_rows.1 = (f32[8,112,768]{2,1,0:T(8,128)}, f32[8,112,640]{2,1,0:T(8,128)}, f32[8,112,384]{2,1,0:T(8,128)}) custom-call(s32[8,1,1792]{2,1,0:T(1,128)S(1)} %bitcast.20, f32[128,104,128]{2,1,0:T(8,128)S(1)} %all_to_all.25.x_ref), custom_call_target="tpu_custom_call" | custom-call | tf_op jit(solution)/shard_map/group_rows/pallas_call | solution.py:109
  127.6 3.6 %all-to-all-start.1 = ((f32[8,112,768]{2,1,0:T(8,128)}), f32[8,112,768]{2,1,0:T(8,128)S(1)}, u32[]{:S(2)}, u32[]{:S(2)}) async-start(f32[8,112,768]{2,1,0:T(8,128)} %get-tuple-element.30), calls=%async_computation.1 | async-start | bytes 5505024 | tf_op jit(solution)/shard_map/all_to_all | solution.py:231
  131.3 0.1 pad_add_fusion.where_ref
  131.4 4.7 %fusion = (bf16[896,1024]{1,0:T(8,128)(2,1)}, bf16[896,1024]{1,0:T(8,128)(2,1)}) fusion(f32[896,1024]{1,0:T(8,128)} %param.5), kind=kLoop, calls=%fused_computation.2 | loop fusion | flops 3670016 | bytes 7340032 | tf_op jit(solution)/shard_map/convert_element_type | solution.py:240
  136.1 29.2 %all-to-all-done.1.x_ref = f32[8,112,768]{2,1,0:T(8,128)S(1)} async-done(((f32[8,112,768]{2,1,0:T(8,128)}), f32[8,112,768]{2,1,0:T(8,128)S(1)}, u32[]{:S(2)}, u32[]{:S(2)}) %all-to-all-start.1) | async-done | bytes 2752544 | tf_op jit(solution)/shard_map/all_to_all | solution.py:231
  165.4 4.4 %all-to-all-start.2 = ((f32[8,112,640]{2,1,0:T(8,128)}), f32[8,112,640]{2,1,0:T(8,128)}, u32[]{:S(2)}, u32[]{:S(2)}) async-start(f32[8,112,640]{2,1,0:T(8,128)} %get-tuple-element.38), calls=%async_computation.2 | async-start | bytes 4587520 | tf_op jit(solution)/shard_map/all_to_all | solution.py:231
  169.7 8.9 %shard_map.50 = (f32[16,112,896]{2,1,0:T(8,128)}, f32[8,48,1024]{2,1,0:T(8,128)S(1)}, f32[8,48,1024]{2,1,0:T(8,128)S(1)}) custom-call(s32[2]{0:T(128)S(1)} %pad_add_fusion.where_ref, f32[8,112,768]{2,1,0:T(8,128)S(1)} %all-to-all-done.1.x_ref, bf16[896,1024]{1,0:T(8,128)(2,1)} %get-tuple-element.57.hi_ref, bf16[896,1024]{1,0:T(8,128)(2,1)} %get-tuple-element.56.lo_ref), custom_call_target="tpu_custom_call" | custom-call | flops 4227858432 | bytes 5505024 | tf_op jit(solution)/shard_map/pallas_call | solution.py:186
  178.7 0.1 collective-permute-start
  178.8 3.4 %collective-permute-done = f32[8,48,1024]{2,1,0:T(8,128)S(1)} collective-permute-done((f32[8,48,1024]{2,1,0:T(8,128)S(1)}, f32[8,48,1024]{2,1,0:T(8,128)S(1)}, u32[]{:S(2)}, u32[]{:S(2)}) %collective-permute-start) | collective-permute-done | bytes 1572896 | tf_op jit(solution)/shard_map/ppermute | solution.py:232
  182.2 1.1 slice_add_fusion
  183.3 0.1 pad_add_fusion.1.where_ref
  183.4 14.7 %all-to-all-done.2.x_ref = f32[8,112,640]{2,1,0:T(8,128)} async-done(((f32[8,112,640]{2,1,0:T(8,128)}), f32[8,112,640]{2,1,0:T(8,128)}, u32[]{:S(2)}, u32[]{:S(2)}) %all-to-all-start.2) | async-done | bytes 2293792 | tf_op jit(solution)/shard_map/all_to_all | solution.py:231
  198.1 9.6 %shard_map.51 = (f32[16,112,896]{2,1,0:T(8,128)}, f32[8,40,1024]{2,1,0:T(8,128)}, f32[8,40,1024]{2,1,0:T(8,128)S(1)}) custom-call(s32[2]{0:T(128)S(1)} %pad_add_fusion.1.where_ref, f32[8,112,640]{2,1,0:T(8,128)} %all-to-all-done.2.x_ref, bf16[896,1024]{1,0:T(8,128)(2,1)} %get-tuple-element.57.hi_ref, ...), custom_call_target="tpu_custom_call", output_to_operand_aliasing={{0}: (4, {})} | custom-call | flops 3523215360 | bytes 4587520 | tf_op jit(solution)/shard_map/pallas_call | solution.py:186
  207.7 0.1 collective-permute-start.1
  207.8 3.6 %all-to-all-start.3 = ((f32[8,112,384]{2,1,0:T(8,128)}), f32[8,112,384]{2,1,0:T(8,128)S(1)}, u32[]{:S(2)}, u32[]{:S(2)}) async-start(f32[8,112,384]{2,1,0:T(8,128)} %get-tuple-element.48), calls=%async_computation.3 | async-start | bytes 2752512 | tf_op jit(solution)/shard_map/all_to_all | solution.py:231
  211.4 0.1 collective-permute-start.2
  211.5 4.0 %collective-permute-start.3 = (f32[2,48,1024]{2,1,0:T(8,128)}, f32[2,48,1024]{2,1,0:T(8,128)}, u32[]{:S(2)}, u32[]{:S(2)}) collective-permute-start(f32[2,48,1024]{2,1,0:T(8,128)} %get-tuple-element.34), channel_id=1, source_target_pairs={{0,8},{1,9},{2,10},{3,11},{4,12},{5,13},{6,14},{7,15},{8,0},{9,1},... | collective-permute-start | bytes 1179656 | tf_op jit(solution)/shard_map/ppermute | solution.py:232
  215.4 0.7 collective-permute-start.4
  216.2 0.0 collective-permute-done.1
  216.2 2.3 slice_add_fusion.4
  218.5 13.0 %all-to-all-done.3.x_ref = f32[8,112,384]{2,1,0:T(8,128)S(1)} async-done(((f32[8,112,384]{2,1,0:T(8,128)}), f32[8,112,384]{2,1,0:T(8,128)S(1)}, u32[]{:S(2)}, u32[]{:S(2)}) %all-to-all-start.3) | async-done | bytes 1376288 | tf_op jit(solution)/shard_map/all_to_all | solution.py:231
  231.5 0.1 pad_add_fusion.2.where_ref
  231.6 5.7 %shard_map.52 = (f32[16,112,896]{2,1,0:T(8,128)}, f32[8,24,1024]{2,1,0:T(8,128)S(1)}, f32[8,24,1024]{2,1,0:T(8,128)S(1)}) custom-call(s32[2]{0:T(128)S(1)} %pad_add_fusion.2.where_ref, f32[8,112,384]{2,1,0:T(8,128)S(1)} %all-to-all-done.3.x_ref, bf16[896,1024]{1,0:T(8,128)(2,1)} %get-tuple-element.57.hi_ref, ...), custom_call_target="tpu_custom_call", output_to_operand_aliasing={{0}: (4, {})} | custom-call | flops 2113929216 | bytes 2752512 | tf_op jit(solution)/shard_map/pallas_call | solution.py:186
  237.3 0.1 collective-permute-start.10
  237.4 0.1 collective-permute-start.6
  237.4 0.0 collective-permute-done.2
  237.5 4.0 %collective-permute-start.7 = (f32[2,40,1024]{2,1,0:T(8,128)S(1)}, f32[2,40,1024]{2,1,0:T(8,128)S(1)}, u32[]{:S(2)}, u32[]{:S(2)}) collective-permute-start(f32[2,40,1024]{2,1,0:T(8,128)S(1)} %copy-done.1), channel_id=1, source_target_pairs={{0,8},{1,9},{2,10},{3,11},{4,12},{5,13},{6,14},{7,15},{8,0},{9,1},... | collective-permute-start | bytes 983048 | tf_op jit(solution)/shard_map/ppermute | solution.py:232
  241.4 0.0 collective-permute-done.3
  241.4 0.7 collective-permute-start.8
  242.1 0.0 collective-permute-done.4
  242.2 1.3 add_add_fusion
  243.5 1.5 collective-permute-start.5
  245.0 3.0 %collective-permute-done.6 = f32[2,40,1024]{2,1,0:T(8,128)S(1)} collective-permute-done((f32[2,40,1024]{2,1,0:T(8,128)S(1)}, f32[2,40,1024]{2,1,0:T(8,128)S(1)}, u32[]{:S(2)}, u32[]{:S(2)}) %collective-permute-start.6) | collective-permute-done | bytes 327712 | tf_op jit(solution)/shard_map/ppermute | solution.py:232
  248.0 8.7 %collective-permute-done.7 = f32[2,40,1024]{2,1,0:T(8,128)S(1)} collective-permute-done((f32[2,40,1024]{2,1,0:T(8,128)S(1)}, f32[2,40,1024]{2,1,0:T(8,128)S(1)}, u32[]{:S(2)}, u32[]{:S(2)}) %collective-permute-start.7) | collective-permute-done | bytes 327712 | tf_op jit(solution)/shard_map/ppermute | solution.py:232
  256.7 2.7 collective-permute-done.8
  259.4 0.1 add_add_fusion.1
  259.5 0.0 collective-permute-done.10
  259.5 1.0 add.164
  260.5 3.5 %all-to-all-start.4 = ((f32[8,24,1024]{2,1,0:T(8,128)}), f32[8,24,1024]{2,1,0:T(8,128)S(1)}, u32[]{:S(2)}, u32[]{:S(2)}) async-start(f32[8,24,1024]{2,1,0:T(8,128)} %add.164), calls=%async_computation.4 | async-start | bytes 1572864 | tf_op jit(solution)/shard_map/all_to_all | solution.py:267
  264.0 3.5 %collective-permute-start.9 = (f32[40,1024]{1,0:T(8,128)S(1)}, f32[40,1024]{1,0:T(8,128)S(1)}, u32[]{:S(2)}, u32[]{:S(2)}) collective-permute-start(f32[40,1024]{1,0:T(8,128)S(1)} %slice_bitcast_fusion.2), channel_id=1, source_target_pairs={{0,2},{1,3},{2,0},{3,1},{4,6},{5,7},{6,4},{7,5},{8,10},{9,11},{10,... | collective-permute-start | bytes 491528 | tf_op jit(solution)/shard_map/ppermute | solution.py:232
  267.5 0.0 collective-permute-done.5
  267.5 0.9 fusion.1
  268.5 10.9 %collective-permute-done.9 = f32[40,1024]{1,0:T(8,128)S(1)} collective-permute-done((f32[40,1024]{1,0:T(8,128)S(1)}, f32[40,1024]{1,0:T(8,128)S(1)}, u32[]{:S(2)}, u32[]{:S(2)}) %collective-permute-start.9) | collective-permute-done | bytes 163872 | tf_op jit(solution)/shard_map/ppermute | solution.py:232
  279.4 0.3 all-to-all-done.4
  279.8 0.8 pad_maximum_fusion
  (10 shorter events, 0.1 us)
Async XLA Ops:
  127.6 37.7 %all-to-all-start.1 = ((f32[8,112,768]{2,1,0:T(8,128)}), f32[8,112,768]{2,1,0:T(8,128)S(1)}, u32[]{:S(2)}, u32[]{:S(2)}) async-start(f32[8,112,768]{2,1,0:T(8,128)} %get-tuple-element.30), calls=%async_computation.1 | async-start | bytes 5505024 | tf_op jit(solution)/shard_map/all_to_all | solution.py:231
  165.4 32.8 %all-to-all-start.2 = ((f32[8,112,640]{2,1,0:T(8,128)}), f32[8,112,640]{2,1,0:T(8,128)}, u32[]{:S(2)}, u32[]{:S(2)}) async-start(f32[8,112,640]{2,1,0:T(8,128)} %get-tuple-element.38), calls=%async_computation.2 | async-start | bytes 4587520 | tf_op jit(solution)/shard_map/all_to_all | solution.py:231
  178.7 3.5 %collective-permute-start = (f32[8,48,1024]{2,1,0:T(8,128)S(1)}, f32[8,48,1024]{2,1,0:T(8,128)S(1)}, u32[]{:S(2)}, u32[]{:S(2)}) collective-permute-start(f32[8,48,1024]{2,1,0:T(8,128)S(1)} %get-tuple-element.32), channel_id=1, source_target_pairs={{0,1},{1,0},{2,3},{3,2},{4,5},{5,4},{6,7},{7,6},{8,9},{9,8},{10,11... | collective-permute-start | bytes 4718600 | tf_op jit(solution)/shard_map/ppermute | solution.py:232
  207.7 8.5 %collective-permute-start.1 = (f32[8,40,1024]{2,1,0:T(8,128)}, f32[8,40,1024]{2,1,0:T(8,128)}, u32[]{:S(2)}, u32[]{:S(2)}) collective-permute-start(f32[8,40,1024]{2,1,0:T(8,128)} %get-tuple-element.42), channel_id=1, source_target_pairs={{0,1},{1,0},{2,3},{3,2},{4,5},{5,4},{6,7},{7,6},{8,9},{9,8},{10,11... | collective-permute-start | bytes 3932168 | tf_op jit(solution)/shard_map/ppermute | solution.py:232
  207.8 23.7 %all-to-all-start.3 = ((f32[8,112,384]{2,1,0:T(8,128)}), f32[8,112,384]{2,1,0:T(8,128)S(1)}, u32[]{:S(2)}, u32[]{:S(2)}) async-start(f32[8,112,384]{2,1,0:T(8,128)} %get-tuple-element.48), calls=%async_computation.3 | async-start | bytes 2752512 | tf_op jit(solution)/shard_map/all_to_all | solution.py:231
  211.4 26.1 %collective-permute-start.2 = (f32[2,48,1024]{2,1,0:T(8,128)}, f32[2,48,1024]{2,1,0:T(8,128)}, u32[]{:S(2)}, u32[]{:S(2)}) collective-permute-start(f32[2,48,1024]{2,1,0:T(8,128)} %get-tuple-element.33), channel_id=1, source_target_pairs={{0,4},{1,5},{2,6},{3,7},{4,0},{5,1},{6,2},{7,3},{8,12},{9,13},{10,... | collective-permute-start | bytes 1179656 | tf_op jit(solution)/shard_map/ppermute | solution.py:232
  211.5 30.0 %collective-permute-start.3 = (f32[2,48,1024]{2,1,0:T(8,128)}, f32[2,48,1024]{2,1,0:T(8,128)}, u32[]{:S(2)}, u32[]{:S(2)}) collective-permute-start(f32[2,48,1024]{2,1,0:T(8,128)} %get-tuple-element.34), channel_id=1, source_target_pairs={{0,8},{1,9},{2,10},{3,11},{4,12},{5,13},{6,14},{7,15},{8,0},{9,1},... | collective-permute-start | bytes 1179656 | tf_op jit(solution)/shard_map/ppermute | solution.py:232
  215.4 26.7 %collective-permute-start.4 = (f32[2,48,1024]{2,1,0:T(8,128)}, f32[2,48,1024]{2,1,0:T(8,128)}, u32[]{:S(2)}, u32[]{:S(2)}) collective-permute-start(f32[2,48,1024]{2,1,0:T(8,128)} %get-tuple-element.35), channel_id=1, source_target_pairs={{0,12},{1,13},{2,14},{3,15},{4,8},{5,9},{6,10},{7,11},{8,4},{9,5},... | collective-permute-start | bytes 1179656 | tf_op jit(solution)/shard_map/ppermute | solution.py:232
  231.6 5.8 %copy-start.2 = (f32[2,40,1024]{2,1,0:T(8,128)S(1)}, f32[2,40,1024]{2,1,0:T(8,128)}, u32[]{:S(2)}) copy-start(f32[2,40,1024]{2,1,0:T(8,128)} %get-tuple-element.43) | copy-start | bytes 983044
  231.6 5.9 %copy-start.1 = (f32[2,40,1024]{2,1,0:T(8,128)S(1)}, f32[2,40,1024]{2,1,0:T(8,128)}, u32[]{:S(2)}) copy-start(f32[2,40,1024]{2,1,0:T(8,128)} %get-tuple-element.44) | copy-start | bytes 983044
  231.6 9.9 %copy-start = (f32[2,40,1024]{2,1,0:T(8,128)S(1)}, f32[2,40,1024]{2,1,0:T(8,128)}, u32[]{:S(2)}) copy-start(f32[2,40,1024]{2,1,0:T(8,128)} %get-tuple-element.45) | copy-start | bytes 983044
  237.3 22.2 %collective-permute-start.10 = (f32[8,24,1024]{2,1,0:T(8,128)S(1)}, f32[8,24,1024]{2,1,0:T(8,128)S(1)}, u32[]{:S(2)}, u32[]{:S(2)}) collective-permute-start(f32[8,24,1024]{2,1,0:T(8,128)S(1)} %get-tuple-element.55), channel_id=1, source_target_pairs={{0,1},{1,0},{2,3},{3,2},{4,5},{5,4},{6,7},{7,6},{8,9},{9,8},{10,11... | collective-permute-start | bytes 2359304 | tf_op jit(solution)/shard_map/ppermute | solution.py:232
  237.4 10.7 %collective-permute-start.6 = (f32[2,40,1024]{2,1,0:T(8,128)S(1)}, f32[2,40,1024]{2,1,0:T(8,128)S(1)}, u32[]{:S(2)}, u32[]{:S(2)}) collective-permute-start(f32[2,40,1024]{2,1,0:T(8,128)S(1)} %copy-done.2), channel_id=1, source_target_pairs={{0,4},{1,5},{2,6},{3,7},{4,0},{5,1},{6,2},{7,3},{8,12},{9,13},{10,... | collective-permute-start | bytes 983048 | tf_op jit(solution)/shard_map/ppermute | solution.py:232
  237.5 19.2 %collective-permute-start.7 = (f32[2,40,1024]{2,1,0:T(8,128)S(1)}, f32[2,40,1024]{2,1,0:T(8,128)S(1)}, u32[]{:S(2)}, u32[]{:S(2)}) collective-permute-start(f32[2,40,1024]{2,1,0:T(8,128)S(1)} %copy-done.1), channel_id=1, source_target_pairs={{0,8},{1,9},{2,10},{3,11},{4,12},{5,13},{6,14},{7,15},{8,0},{9,1},... | collective-permute-start | bytes 983048 | tf_op jit(solution)/shard_map/ppermute | solution.py:232
  241.4 18.0 %collective-permute-start.8 = (f32[2,40,1024]{2,1,0:T(8,128)S(1)}, f32[2,40,1024]{2,1,0:T(8,128)S(1)}, u32[]{:S(2)}, u32[]{:S(2)}) collective-permute-start(f32[2,40,1024]{2,1,0:T(8,128)S(1)} %copy-done), channel_id=1, source_target_pairs={{0,12},{1,13},{2,14},{3,15},{4,8},{5,9},{6,10},{7,11},{8,4},{9,5},... | collective-permute-start | bytes 983048 | tf_op jit(solution)/shard_map/ppermute | solution.py:232
  243.5 24.0 %collective-permute-start.5 = (f32[48,1024]{1,0:T(8,128)S(1)}, f32[48,1024]{1,0:T(8,128)}, u32[]{:S(2)}, u32[]{:S(2)}) collective-permute-start(f32[48,1024]{1,0:T(8,128)S(1)} %slice_bitcast_fusion), channel_id=1, source_target_pairs={{0,2},{1,3},{2,0},{3,1},{4,6},{5,7},{6,4},{7,5},{8,10},{9,11},{10,... | collective-permute-start | bytes 589832 | tf_op jit(solution)/shard_map/ppermute | solution.py:232
  260.5 19.3 %all-to-all-start.4 = ((f32[8,24,1024]{2,1,0:T(8,128)}), f32[8,24,1024]{2,1,0:T(8,128)S(1)}, u32[]{:S(2)}, u32[]{:S(2)}) async-start(f32[8,24,1024]{2,1,0:T(8,128)} %add.164), calls=%async_computation.4 | async-start | bytes 1572864 | tf_op jit(solution)/shard_map/all_to_all | solution.py:267
  264.0 15.4 %collective-permute-start.9 = (f32[40,1024]{1,0:T(8,128)S(1)}, f32[40,1024]{1,0:T(8,128)S(1)}, u32[]{:S(2)}, u32[]{:S(2)}) collective-permute-start(f32[40,1024]{1,0:T(8,128)S(1)} %slice_bitcast_fusion.2), channel_id=1, source_target_pairs={{0,2},{1,3},{2,0},{3,1},{4,6},{5,7},{6,4},{7,5},{8,10},{9,11},{10,... | collective-permute-start | bytes 491528 | tf_op jit(solution)/shard_map/ppermute | solution.py:232
